TPU v7x, 32 devices: a whole 2x2x4 slice. The times are simulated.
32 devices in a mesh: cand: 4 (over y, core), tensor: 8 (over z, x).
Axes of the slice: x: 2, y: 2, z: 4, core: 2. Of those that a mesh axis runs over, the one named last changes fastest.
Arguments:
- states: bfloat16 [512, 3584], P('cand'), may hold values from -60 to 60
- targets: int32 [512], replicated, may hold values from 0 to 131071
- loss_mask: int32 [512], P('cand'), may hold values 0 or 1
- cand_of: int32 [4], replicated, may hold values from 0 to 3
- lambdas: float32 [4], replicated, may hold values from 0.2 to 1
- base_q: bfloat16 [3584, 4096], P('cand', 'tensor'), may hold values from -0.09375 to 0.09375
- delta_q: bfloat16 [2, 3584, 4096], P(None, 'cand', 'tensor'), may hold values from -0.046875 to 0.046875
- base_k: bfloat16 [3584, 2048], P('cand'), may hold values from -0.09375 to 0.09375
- delta_k: bfloat16 [2, 3584, 2048], P(None, 'cand'), may hold values from -0.046875 to 0.046875
- base_v: bfloat16 [3584, 2048], P('cand'), may hold values from -0.09375 to 0.09375
- delta_v: bfloat16 [2, 3584, 2048], P(None, 'cand'), may hold values from -0.046875 to 0.046875
- base_o: bfloat16 [4096, 3584], P('tensor', 'cand'), may hold values from -0.09375 to 0.09375
- delta_o: bfloat16 [2, 4096, 3584], P(None, 'tensor', 'cand'), may hold values from -0.046875 to 0.046875
- pre_gain: float32 [3584], replicated, may hold values from 0.5 to 2
- post_gain: float32 [3584], replicated, may hold values from 0.5 to 2
- final_gain: float32 [3584], replicated, may hold values from 0.5 to 2
- unembed: bfloat16 [3584, 131072], P(None, ('cand', 'tensor')), may hold values from -0.3125 to 0.3125
Outputs:
- token_loss: float32 [512], P('cand')
- cand_loss: float32 [4], replicated
All inputs are finite; a program needn't handle non-finite values. No bound on the sum of `loss_mask` on one device may be relied on, other than what follows from the above.
Results may differ from a plain program's by a relative error of at most 0.002.
Values may be sent and summed in bfloat16 or wider, within the bound.
No kernel may reach another device: no remote copies, remote signals or barrier semaphores. Data moves between devices by JAX's collectives and lax.ppermute only.
A program may use at most 128 MiB of HBM per device.

v0:
```python
import math
import jax
import jax.numpy as jnp
from jax import lax
from jax.sharding import PartitionSpec as P

KV = 8
HEAD_SIZE = 256
CANDS = 4


def root_norm(entries, scale_gain):
    mean_square = jnp.mean(entries * entries, axis=-1, keepdims=True)
    return entries * lax.rsqrt(mean_square + 1e-06) * scale_gain


def rotate_pairs(entries, length):
    half_width = entries.shape[-1] // 2
    positions = jnp.arange(length).astype(jnp.float32)
    frequency = jnp.exp(
        -math.log(10000.0) * jnp.arange(half_width).astype(jnp.float32) * 2.0 / entries.shape[-1]
    )
    angles = positions[:, None] * frequency[None, :]
    cosine = jnp.cos(angles)[:, None, :]
    sine_part = jnp.sin(angles)[:, None, :]
    first = entries[..., :half_width]
    second = entries[..., half_width:]
    return jnp.concatenate(
        [first * cosine - second * sine_part, second * cosine + first * sine_part], axis=-1
    )


def task_total(delta):
    return jnp.sum(delta.astype(jnp.float32), axis=0).astype(jnp.bfloat16)


def merge_weights(base, total, mixing):
    return (base.astype(jnp.float32) + mixing * total.astype(jnp.float32)).astype(jnp.bfloat16)


def on_device(
    states,
    targets,
    loss_mask,
    cand_of,
    lambdas,
    base_q,
    delta_q,
    base_k,
    delta_k,
    base_v,
    delta_v,
    base_o,
    delta_o,
    pre_gain,
    post_gain,
    final_gain,
    unembed,
):
    cand_id = lax.axis_index("cand")
    tensor_id = lax.axis_index("tensor")
    tensor_count = lax.axis_size("tensor")
    chosen = cand_of[cand_id]
    mixing = lambdas[chosen]
    group_size = tensor_count // KV
    head_start = tensor_id // group_size * HEAD_SIZE
    own_base_k = lax.dynamic_slice_in_dim(base_k, head_start, HEAD_SIZE, 1)
    own_base_v = lax.dynamic_slice_in_dim(base_v, head_start, HEAD_SIZE, 1)
    own_delta_k = lax.dynamic_slice_in_dim(delta_k, head_start, HEAD_SIZE, 2)
    own_delta_v = lax.dynamic_slice_in_dim(delta_v, head_start, HEAD_SIZE, 2)
    summed = [task_total(delta) for delta in (delta_q, own_delta_k, own_delta_v, delta_o)]
    pieces = (
        lax.all_gather(base_q, "cand", axis=0, tiled=True),
        lax.all_gather(own_base_k, "cand", axis=0, tiled=True),
        lax.all_gather(own_base_v, "cand", axis=0, tiled=True),
        lax.all_gather(base_o, "cand", axis=1, tiled=True),
        lax.all_gather(summed[0], "cand", axis=0, tiled=True),
        lax.all_gather(summed[1], "cand", axis=0, tiled=True),
        lax.all_gather(summed[2], "cand", axis=0, tiled=True),
        lax.all_gather(summed[3], "cand", axis=1, tiled=True),
    )
    base_parts = pieces[:4]
    task_parts = pieces[4:]
    w_query = merge_weights(base_parts[0], task_parts[0], mixing)
    w_key = merge_weights(base_parts[1], task_parts[1], mixing)
    w_value = merge_weights(base_parts[2], task_parts[2], mixing)
    w_out = merge_weights(base_parts[3], task_parts[3], mixing)
    length = states.shape[0]
    stream = states.astype(jnp.float32)
    normed = root_norm(stream, pre_gain).astype(jnp.bfloat16)
    query_rows = jnp.dot(normed, w_query, preferred_element_type=jnp.float32).reshape(
        length, -1, HEAD_SIZE
    )
    query_rows = rotate_pairs(query_rows, length).astype(jnp.bfloat16)
    key_full = jnp.dot(normed, w_key, preferred_element_type=jnp.float32).astype(jnp.bfloat16)
    value_full = jnp.dot(normed, w_value, preferred_element_type=jnp.float32).astype(jnp.bfloat16)
    key_matrix = rotate_pairs(
        key_full.astype(jnp.float32).reshape(length, 1, HEAD_SIZE), length
    ).astype(jnp.bfloat16)[:, 0, :]
    attention_scores = jnp.einsum(
        "lhd,md->hlm", query_rows, key_matrix, preferred_element_type=jnp.float32
    ) * HEAD_SIZE ** (-0.5)
    attention_scores = 50.0 * jnp.tanh(attention_scores / 50.0)
    causal = jnp.arange(length)[:, None] >= jnp.arange(length)[None, :]
    weights = jnp.where(causal[None, :, :], jnp.exp(attention_scores), 0.0)
    attention_probs = (weights / jnp.sum(weights, axis=-1, keepdims=True)).astype(jnp.bfloat16)
    context_rows = jnp.einsum(
        "hlm,md->lhd", attention_probs, value_full, preferred_element_type=jnp.float32
    )
    context_rows = context_rows.astype(jnp.bfloat16).reshape(length, -1)
    partial_value = jnp.dot(context_rows, w_out, preferred_element_type=jnp.float32)
    vocab_width = unembed.shape[1]
    vocab_start = (cand_id * tensor_count + tensor_id) * vocab_width
    vocab_index = jnp.arange(vocab_width)
    attended = lax.psum(partial_value, "tensor")
    final_rows = root_norm(stream + root_norm(attended, post_gain), final_gain).astype(jnp.bfloat16)
    logits = jnp.dot(
        lax.all_gather(final_rows, "cand", axis=0, tiled=True),
        unembed,
        preferred_element_type=jnp.float32,
    )
    capped = 30.0 * jnp.tanh(logits / 30.0)
    totals = jnp.sum(jnp.exp(capped), axis=1)
    local_ids = targets - vocab_start
    matches = local_ids[:, None] == vocab_index[None, :]
    picked = jnp.sum(jnp.where(matches, capped, 0.0), axis=1)
    vocab_sums = jnp.stack([totals, picked], axis=0)
    summed_terms = lax.psum(vocab_sums, ("cand", "tensor"))
    own_terms = lax.dynamic_slice_in_dim(summed_terms, cand_id * length, length, 1)
    mask_values = loss_mask.astype(jnp.float32)
    token_loss = mask_values * (jnp.log(own_terms[0]) - own_terms[1])
    onehot = (chosen == jnp.arange(CANDS)).astype(jnp.float32)
    loss_sums, counts = lax.psum(
        (onehot * jnp.sum(token_loss), onehot * jnp.sum(mask_values)), "cand"
    )
    return (token_loss, loss_sums / jnp.maximum(counts, 1.0))


def solution(mesh):
    in_specs = (
        P("cand", None),
        P(),
        P("cand"),
        P(),
        P(),
        P("cand", "tensor"),
        P(None, "cand", "tensor"),
        P("cand", None),
        P(None, "cand", None),
        P("cand", None),
        P(None, "cand", None),
        P("tensor", "cand"),
        P(None, "tensor", "cand"),
        P(),
        P(),
        P(),
        P(None, ("cand", "tensor")),
    )
    out_specs = (P("cand"), P())
    return jax.shard_map(
        on_device, mesh=mesh, in_specs=in_specs, out_specs=out_specs, check_vma=False
    )
```

profile of v0, /device:TPU:0, one launch (start us, length us, event | category | flops | bytes accessed | tf_op | source)
XLA Modules:
  0.0 451.5 jit_solution(439209231556427896)
XLA Ops:
  7.2 1.9 constant_dynamic-slice_fusion.1
  9.2 2.3 dynamic-slice_reduce_fusion
  11.6 1.6 reduce_sum.123
  13.2 0.5 all-gather.18.cloned.1.call-update
  13.8 1.8 constant_dynamic-slice_fusion.2
  15.7 2.4 dynamic-slice_reduce_fusion.1
  18.2 1.5 reduce_sum.125
  19.8 0.7 all-gather.22.cloned.1.call-update
  20.6 0.6 dynamic_slice.22
  23.1 0.6 dynamic_slice.23
  24.3 9.1 %all-gather.14.cloned.1.call-done = bf16[3584,256]{1,0:T(8,128)(2,1)} async-done(((bf16[896,256]{1,0:T(8,128)(2,1)}), bf16[3584,256]{1,0:T(8,128)(2,1)}) %all-gather.14.cloned.1.call-update) | async-done | bytes 1835024 | tf_op jit(solution)/shard_map/all_gather | solution.py:74
  33.4 22.7 %all-gather.16.cloned.1.call-done = bf16[3584,256]{1,0:T(8,128)(2,1)} async-done(((bf16[896,256]{1,0:T(8,128)(2,1)}), bf16[3584,256]{1,0:T(8,128)(2,1)}) %all-gather.16.cloned.1.call-update) | async-done | bytes 1835024 | tf_op jit(solution)/shard_map/all_gather | solution.py:78
  56.1 3.6 fusion.20
  60.0 29.2 %all-gather.20.cloned.1.call-done = bf16[3584,512]{1,0:T(8,128)(2,1)} async-done(((bf16[896,512]{1,0:T(8,128)(2,1)}), bf16[3584,512]{1,0:T(8,128)(2,1)}) %all-gather.20.cloned.1.call-update) | async-done | bytes 3670032 | tf_op jit(solution)/shard_map/all_gather | solution.py:77
  89.2 32.9 %all-gather.18.cloned.1.call-done = bf16[3584,512]{1,0:T(8,128)(2,1)} async-done(((bf16[896,512]{1,0:T(8,128)(2,1)}), bf16[3584,512]{1,0:T(8,128)(2,1)}) %all-gather.18.cloned.1.call-update) | async-done | bytes 3670032 | tf_op jit(solution)/shard_map/all_gather | solution.py:73
  122.1 5.2 %fusion = f32[128,512]{1,0:T(8,128)S(1)} fusion(bf16[3584,512]{1,0:T(8,128)(2,1)} %all-gather.20.cloned.1.call-done, bf16[3584,512]{1,0:T(8,128)(2,1)} %all-gather.18.cloned.1.call-done, f32[]{:T(128)} %bitcast.1, bf16[128,3584]{1,0:T(8,128)(2,1)S(1)} %copy-done.1, f32[3584]{0:T(1024)S(1)} %copy-done.8, f32[128]{0:T(128)S(1)} %add_rsqrt_fusion.2), kind=kOutput, calls=%fused_computation.6 | convolution fusion | flops 480772096 | bytes 8534532 | tf_op jit(solution)/shard_map/dot_general | solution.py:91
  127.9 16.7 %all-gather.10.cloned.1.call-done = bf16[3584,256]{1,0:T(8,128)(2,1)} async-done(((bf16[896,256]{1,0:T(8,128)(2,1)}), bf16[3584,256]{1,0:T(8,128)(2,1)}) %all-gather.10.cloned.1.call-update) | async-done | bytes 1835024 | tf_op jit(solution)/shard_map/all_gather | solution.py:75
  144.6 22.5 %all-gather.12.cloned.1.call-done = bf16[3584,256]{1,0:T(8,128)(2,1)} async-done(((bf16[896,256]{1,0:T(8,128)(2,1)}), bf16[3584,256]{1,0:T(8,128)(2,1)}) %all-gather.12.cloned.1.call-update) | async-done | bytes 1835024 | tf_op jit(solution)/shard_map/all_gather | solution.py:79
  167.2 3.9 convolution_convert_fusion
  171.1 29.1 %all-gather.24.cloned.1.call-done = bf16[512,3584]{1,0:T(8,128)(2,1)} async-done(((bf16[512,896]{1,0:T(8,128)(2,1)}), bf16[512,3584]{1,0:T(8,128)(2,1)}) %all-gather.24.cloned.1.call-update) | async-done | bytes 3670032 | tf_op jit(solution)/shard_map/all_gather | solution.py:80
  200.2 33.1 %all-gather.22.cloned.1.call-done = bf16[512,3584]{1,0:T(8,128)(2,1)} async-done(((bf16[512,896]{1,0:T(8,128)(2,1)}), bf16[512,3584]{1,0:T(8,128)(2,1)}) %all-gather.22.cloned.1.call-update) | async-done | bytes 3670032 | tf_op jit(solution)/shard_map/all_gather | solution.py:76
  233.3 6.6 %fusion.1 = f32[128,3584]{1,0:T(8,128)} fusion(bf16[128,512]{0,1:T(8,128)(2,1)S(1)} %bitcast.38, bf16[512,3584]{1,0:T(8,128)(2,1)} %all-gather.24.cloned.1.call-done, bf16[512,3584]{1,0:T(8,128)(2,1)} %all-gather.22.cloned.1.call-done, f32[]{:T(128)} %bitcast.1), kind=kOutput, calls=%fused_computation.7 | convolution fusion | flops 478937088 | bytes 9306116 | tf_op jit(solution)/shard_map/dot_general | solution.py:111
  240.2 95.7 %all-reduce.3.cloned.1.call-done = f32[128,3584]{1,0:T(8,128)} async-done(((f32[128,3584]{1,0:T(8,128)}), f32[128,3584]{1,0:T(8,128)}) %all-reduce.3.cloned.1.call-update) | async-done | bytes 1835024 | tf_op jit(solution)/shard_map/psum | solution.py:115
  335.9 1.8 multiply_reduce_fusion.1
  337.8 2.0 multiply_reduce_fusion
  339.8 1.4 multiply_convert_fusion
  341.3 31.1 %all-gather.26.cloned.1.call-done = bf16[512,3584]{1,0:T(8,128)(2,1)} async-done(((bf16[128,3584]{1,0:T(8,128)(2,1)}), bf16[512,3584]{1,0:T(8,128)(2,1)}) %all-gather.26.cloned.1.call-update) | async-done | bytes 3670032 | tf_op jit(solution)/shard_map/all_gather | solution.py:118
  372.4 22.9 %exponential_reduce_fusion = (f32[512]{0:T(512)S(1)}, f32[512]{0:T(512)S(1)}) fusion(s32[512]{0:T(512)S(1)} %broadcast_subtract_fusion, bf16[512,3584]{1,0:T(8,128)(2,1)} %all-gather.26.cloned.1.call-done, bf16[3584,4096]{1,0:T(8,128)(2,1)} %param.33), kind=kOutput, calls=%fused_computation.2 | convolution fusion | flops 15044968448 | bytes 33036288 | tf_op jit(solution)/shard_map/dot_general | solution.py:117
  395.3 39.3 %psum.29 = f32[2,512]{1,0:T(2,128)S(1)} all-reduce(f32[2,512]{1,0:T(2,128)S(1)} %pad_maximum_fusion), channel_id=1, replica_groups=mesh['cand'=4,'tensor'=8] {'cand','tensor'}, use_global_device_ids=true, to_apply=%region_11.12 | all-reduce | flops 1024 | bytes 8192 | tf_op jit(solution)/shard_map/psum | solution.py:128
  434.7 1.1 fusion.52
  435.8 1.8 compare_select_fusion
  437.6 6.5 %all-reduce = (f32[4]{0:T(128)S(1)}, f32[4]{0:T(128)S(1)}) all-reduce(f32[4]{0:T(128)S(1)} %get-tuple-element.18, f32[4]{0:T(128)S(1)} %get-tuple-element.17), channel_id=1, replica_groups=mesh['cand'=4,'tensor'=8] {'cand'}, use_global_device_ids=true, to_apply=%region_13.14 | all-reduce | flops 8 | bytes 64 | tf_op jit(solution)/shard_map/psum | solution.py:133
  (57 shorter events, 2.8 us)
Async XLA Ops:
  7.2 4.4 copy-start.2
  7.2 26.2 %all-gather.14.cloned.1.call-start = ((), (), s32[]{:S(2)}) async-start(), calls=%async_computation.2 | async-start | bytes 2293760 | tf_op jit(solution)/shard_map/all_gather | solution.py:74
  9.2 46.9 %all-gather.16.cloned.1.call-start = ((), (), s32[]{:S(2)}) async-start(), calls=%async_computation.3 | async-start | bytes 2293760 | tf_op jit(solution)/shard_map/all_gather | solution.py:78
  11.6 77.6 %all-gather.20.cloned.1.call-start = ((), (), s32[]{:S(2)}) async-start(), calls=%async_computation.5 | async-start | bytes 4587520 | tf_op jit(solution)/shard_map/all_gather | solution.py:77
  13.2 5.0 %copy-start.3 = (bf16[2,512,896]{2,1,0:T(8,128)(2,1)S(1)}, bf16[2,512,896]{2,1,0:T(8,128)(2,1)}, u32[]{:S(2)}) copy-start(bf16[2,512,896]{2,1,0:T(8,128)(2,1)} %param.29) | copy-start | bytes 5505028
  13.2 108.9 %all-gather.18.cloned.1.call-start = ((), (), s32[]{:S(2)}) async-start(), calls=%async_computation.4 | async-start | bytes 4587520 | tf_op jit(solution)/shard_map/all_gather | solution.py:73
  13.8 130.9 %all-gather.10.cloned.1.call-start = ((), (), s32[]{:S(2)}) async-start(), calls=%async_computation | async-start | bytes 2293760 | tf_op jit(solution)/shard_map/all_gather | solution.py:75
  15.6 4.9 %copy-start.9 = (s32[4]{0:T(128)S(1)}, s32[4]{0:T(128)}, u32[]{:S(2)}) copy-start(s32[4]{0:T(128)} %param.20) | copy-start | bytes 52
  15.6 7.4 %copy-start.10 = (f32[4]{0:T(128)S(1)}, f32[4]{0:T(128)}, u32[]{:S(2)}) copy-start(f32[4]{0:T(128)} %param.21) | copy-start | bytes 52
  15.7 8.1 %copy-start.1 = (bf16[128,3584]{1,0:T(8,128)(2,1)S(1)}, bf16[128,3584]{1,0:T(8,128)(2,1)}, u32[]{:S(2)}) copy-start(bf16[128,3584]{1,0:T(8,128)(2,1)} %param.17) | copy-start | bytes 2752516
  15.7 40.4 %copy-start.8 = (f32[3584]{0:T(1024)S(1)}, f32[3584]{0:T(1024)}, u32[]{:S(2)}) copy-start(f32[3584]{0:T(1024)} %param.30) | copy-start | bytes 43012
  15.7 151.5 %all-gather.12.cloned.1.call-start = ((), (), s32[]{:S(2)}) async-start(), calls=%async_computation.1 | async-start | bytes 2293760 | tf_op jit(solution)/shard_map/all_gather | solution.py:79
  18.2 182.1 %all-gather.24.cloned.1.call-start = ((), (), s32[]{:S(2)}) async-start(), calls=%async_computation.7 | async-start | bytes 4587520 | tf_op jit(solution)/shard_map/all_gather | solution.py:80
  19.7 213.6 %all-gather.22.cloned.1.call-start = ((), (), s32[]{:S(2)}) async-start(), calls=%async_computation.6 | async-start | bytes 4587520 | tf_op jit(solution)/shard_map/all_gather | solution.py:76
  20.5 315.4 %all-reduce.3.cloned.1.call-start = ((), (), s32[]{:S(2)}) async-start(), calls=%async_computation.8 | async-start | bytes 3670016 | tf_op jit(solution)/shard_map/psum | solution.py:115
  239.9 97.8 %copy-start.4 = (f32[3584]{0:T(1024)S(1)}, f32[3584]{0:T(1024)}, u32[]{:S(2)}) copy-start(f32[3584]{0:T(1024)} %param.31) | copy-start | bytes 43012
  239.9 99.9 %copy-start.5 = (f32[3584]{0:T(1024)S(1)}, f32[3584]{0:T(1024)}, u32[]{:S(2)}) copy-start(f32[3584]{0:T(1024)} %param.32) | copy-start | bytes 43012
  239.9 132.5 %all-gather.26.cloned.1.call-start = ((), (), s32[]{:S(2)}) async-start(), calls=%async_computation.9 | async-start | bytes 4587520 | tf_op jit(solution)/shard_map/all_gather | solution.py:118
  335.9 3.9 copy-start
  337.8 3.5 copy-start.6
  341.3 93.4 %copy-start.7 = (s32[128]{0:T(128)S(1)}, s32[128]{0:T(128)}, u32[]{:S(2)}) copy-start(s32[128]{0:T(128)} %param.19) | copy-start | bytes 1540
Sparse Core Ops, SparseCore 0:
  9.5 23.8 all-gather.13
  35.0 21.0 all-gather.15
  57.7 31.4 all-gather.19
  90.6 31.4 all-gather.17
  123.5 21.0 all-gather.9
  146.1 21.0 all-gather.11
  168.7 31.4 all-gather.23
  201.8 31.4 all-gather.21
  240.1 95.7 all-reduce.2
  341.4 30.9 all-gather.25
where the time goes:
time: 452 us
  waiting for transfers between devices  324 us (72%)
  blocking collectives  45.9 us (10%)
  matrix products  42.5 us (9%)
  other arithmetic  17.5 us (4%)
  between operations  16.3 us (4%)
  local copies, waits for them, and re-layouts  5.26 us (1%)
    psum x1, waiting for transfers between devices, on_device(): attended = lax.psum(partial_value, 'tensor')  95.7 us
    psum x1, blocking collectives, on_device(): summed_terms = lax.psum(vocab_sums, ('cand', 'tensor'))  39.3 us
    all_gather x1, waiting for transfers between devices, on_device(): lax.all_gather(base_o, 'cand', axis=1, tiled=True)  33.1 us
    all_gather x1, waiting for transfers between devices, on_device(): lax.all_gather(base_q, 'cand', axis=0, tiled=True)  32.9 us
    all_gather x1, waiting for transfers between devices, on_device(): lax.all_gather(final_rows, 'cand', axis=0, tiled=True)  31.1 us
    all_gather x1, waiting for transfers between devices, on_device(): lax.all_gather(summed[0], 'cand', axis=0, tiled=True)  29.2 us
    all_gather x1, waiting for transfers between devices, on_device(): lax.all_gather(summed[3], 'cand', axis=1, tiled=True)  29.1 us
    dot_general x1, matrix products, on_device(): jnp.dot(lax.all_gather(final_rows, 'cand', axis=0, tiled=True), unembed,...  22.9 us
  transfers between devices with their start and end apart: 10, of which 10 were waited for; matrix products, arithmetic and copies ran while one was open for 6% of the time, Pallas kernels for 0%

commit v1 on v0

--- a/solution.py
+++ b/solution.py
@@ -3,6 +3,7 @@
 import jax.numpy as jnp
 from jax import lax
 from jax.sharding import PartitionSpec as P
+from jax.lax import all_gather
 
 KV = 8
 HEAD_SIZE = 256
@@ -112,7 +113,7 @@
     vocab_width = unembed.shape[1]
     vocab_start = (cand_id * tensor_count + tensor_id) * vocab_width
     vocab_index = jnp.arange(vocab_width)
-    attended = lax.psum(partial_value, "tensor")
+    attended = all_gather(partial_value, axis_name="tensor").sum(axis=0)
     final_rows = root_norm(stream + root_norm(attended, post_gain), final_gain).astype(jnp.bfloat16)
     logits = jnp.dot(
         lax.all_gather(final_rows, "cand", axis=0, tiled=True),

time: 452 us -> 560 us (1.24)
  waiting for transfers between devices: 324 us -> 428 us
    all_gather x0 -> x1, waiting for transfers between devices: none -> 202 us  [on_device(): attended = all_gather(partial_value, axis_name='tensor').sum(axis=0)]
    psum x1 -> x0, waiting for transfers between devices: 95.7 us -> none  [on_device(): attended = lax.psum(partial_value, 'tensor')]
    reduce_sum x0 -> x1, other arithmetic: none -> 6.63 us  [on_device(): attended = all_gather(partial_value, axis_name='tensor').sum(axis=0)]
  transfers between devices with their start and end apart: 10 -> 10, of which waited for: 10 -> 10; matrix products, arithmetic and copies ran while one was open for 6% -> 4% of each run, Pallas kernels for 0% -> 0%
where the time goes in v1:
time: 560 us
  waiting for transfers between devices  428 us (76%)
  blocking collectives  45.9 us (8%)
  matrix products  42.4 us (8%)
  other arithmetic  21 us (4%)
  between operations  16.3 us (3%)
    all_gather x1, waiting for transfers between devices, on_device(): attended = all_gather(partial_value, axis_name='tensor').sum(axis=0)  202 us
    psum x1, blocking collectives, on_device(): summed_terms = lax.psum(vocab_sums, ('cand', 'tensor'))  39.3 us
    all_gather x1, waiting for transfers between devices, on_device(): lax.all_gather(base_o, 'cand', axis=1, tiled=True)  33.1 us
    all_gather x1, waiting for transfers between devices, on_device(): lax.all_gather(base_q, 'cand', axis=0, tiled=True)  32.9 us
    all_gather x1, waiting for transfers between devices, on_device(): lax.all_gather(final_rows, 'cand', axis=0, tiled=True)  29.8 us
    all_gather x1, waiting for transfers between devices, on_device(): lax.all_gather(summed[0], 'cand', axis=0, tiled=True)  29.2 us
    all_gather x1, waiting for transfers between devices, on_device(): lax.all_gather(summed[3], 'cand', axis=1, tiled=True)  29.1 us
    dot_general x1, matrix products, on_device(): jnp.dot(lax.all_gather(final_rows, 'cand', axis=0, tiled=True), unembed,...  22.9 us
  transfers between devices with their start and end apart: 10, of which 10 were waited for; matrix products, arithmetic and copies ran while one was open for 4% of the time, Pallas kernels for 0%

profile of v1, /device:TPU:0, one launch (start us, length us, event | category | flops | bytes accessed | tf_op | source)
XLA Modules:
  0.0 559.5 jit_solution(8946879134665706387)
XLA Ops:
  7.2 1.9 constant_dynamic-slice_fusion.1
  9.2 2.3 dynamic-slice_reduce_fusion
  11.6 1.5 reduce_sum.132
  13.2 0.5 all-gather.20.cloned.1.call-update
  13.8 1.8 constant_dynamic-slice_fusion.2
  15.7 2.4 dynamic-slice_reduce_fusion.1
  18.2 1.5 reduce_sum.134
  19.7 0.7 all-gather.24.cloned.1.call-update
  20.5 0.6 dynamic_slice.22
  23.0 0.6 dynamic_slice.23
  24.3 9.1 %all-gather.16.cloned.1.call-done = bf16[3584,256]{1,0:T(8,128)(2,1)} async-done(((bf16[896,256]{1,0:T(8,128)(2,1)}), bf16[3584,256]{1,0:T(8,128)(2,1)}) %all-gather.16.cloned.1.call-update) | async-done | bytes 1835024 | tf_op jit(solution)/shard_map/all_gather | solution.py:75
  33.4 22.7 %all-gather.18.cloned.1.call-done = bf16[3584,256]{1,0:T(8,128)(2,1)} async-done(((bf16[896,256]{1,0:T(8,128)(2,1)}), bf16[3584,256]{1,0:T(8,128)(2,1)}) %all-gather.18.cloned.1.call-update) | async-done | bytes 1835024 | tf_op jit(solution)/shard_map/all_gather | solution.py:79
  56.1 3.6 fusion.20
  60.0 29.2 %all-gather.22.cloned.1.call-done = bf16[3584,512]{1,0:T(8,128)(2,1)} async-done(((bf16[896,512]{1,0:T(8,128)(2,1)}), bf16[3584,512]{1,0:T(8,128)(2,1)}) %all-gather.22.cloned.1.call-update) | async-done | bytes 3670032 | tf_op jit(solution)/shard_map/all_gather | solution.py:78
  89.2 32.9 %all-gather.20.cloned.1.call-done = bf16[3584,512]{1,0:T(8,128)(2,1)} async-done(((bf16[896,512]{1,0:T(8,128)(2,1)}), bf16[3584,512]{1,0:T(8,128)(2,1)}) %all-gather.20.cloned.1.call-update) | async-done | bytes 3670032 | tf_op jit(solution)/shard_map/all_gather | solution.py:74
  122.1 5.2 fusion
  127.9 16.7 %all-gather.12.cloned.1.call-done = bf16[3584,256]{1,0:T(8,128)(2,1)} async-done(((bf16[896,256]{1,0:T(8,128)(2,1)}), bf16[3584,256]{1,0:T(8,128)(2,1)}) %all-gather.12.cloned.1.call-update) | async-done | bytes 1835024 | tf_op jit(solution)/shard_map/all_gather | solution.py:76
  144.6 22.5 %all-gather.14.cloned.1.call-done = bf16[3584,256]{1,0:T(8,128)(2,1)} async-done(((bf16[896,256]{1,0:T(8,128)(2,1)}), bf16[3584,256]{1,0:T(8,128)(2,1)}) %all-gather.14.cloned.1.call-update) | async-done | bytes 1835024 | tf_op jit(solution)/shard_map/all_gather | solution.py:80
  167.2 3.9 convolution_convert_fusion
  171.1 29.1 %all-gather.26.cloned.1.call-done = bf16[512,3584]{1,0:T(8,128)(2,1)} async-done(((bf16[512,896]{1,0:T(8,128)(2,1)}), bf16[512,3584]{1,0:T(8,128)(2,1)}) %all-gather.26.cloned.1.call-update) | async-done | bytes 3670032 | tf_op jit(solution)/shard_map/all_gather | solution.py:81
  200.2 33.1 %all-gather.24.cloned.1.call-done = bf16[512,3584]{1,0:T(8,128)(2,1)} async-done(((bf16[512,896]{1,0:T(8,128)(2,1)}), bf16[512,3584]{1,0:T(8,128)(2,1)}) %all-gather.24.cloned.1.call-update) | async-done | bytes 3670032 | tf_op jit(solution)/shard_map/all_gather | solution.py:77
  233.3 6.5 %fusion.1 = f32[128,3584]{1,0:T(8,128)} fusion(bf16[128,512]{0,1:T(8,128)(2,1)S(1)} %bitcast.40, bf16[512,3584]{1,0:T(8,128)(2,1)} %all-gather.26.cloned.1.call-done, bf16[512,3584]{1,0:T(8,128)(2,1)} %all-gather.24.cloned.1.call-done, f32[]{:T(128)} %bitcast.1), kind=kOutput, calls=%fused_computation.7 | convolution fusion | flops 478937088 | bytes 9306116 | tf_op jit(solution)/shard_map/dot_general | solution.py:112
  240.1 201.6 %all-gather.30.cloned.1.call-done = f32[1024,3584]{1,0:T(8,128)} async-done(((f32[128,3584]{1,0:T(8,128)}), f32[1024,3584]{1,0:T(8,128)}) %all-gather.30.cloned.1.call-update) | async-done | bytes 14680080 | tf_op jit(solution)/shard_map/all_gather | solution.py:116
  441.7 6.6 %reduce_sum.135 = f32[128,3584]{1,0:T(8,128)S(1)} reduce(f32[8,128,3584]{2,1,0:T(8,128)} %bitcast.39, f32[]{:T(128)} %constant.50.clone.1), dimensions={0}, to_apply=%region_6.7 | reduce | flops 3211264 | bytes 16515076 | tf_op jit(solution)/shard_map/reduce_sum | solution.py:116
  449.1 1.4 multiply_convert_fusion
  450.5 29.8 %all-gather.28.cloned.1.call-done = bf16[512,3584]{1,0:T(8,128)(2,1)} async-done(((bf16[128,3584]{1,0:T(8,128)(2,1)}), bf16[512,3584]{1,0:T(8,128)(2,1)}) %all-gather.28.cloned.1.call-update) | async-done | bytes 3670032 | tf_op jit(solution)/shard_map/all_gather | solution.py:119
  480.3 22.9 %exponential_reduce_fusion = (f32[512]{0:T(512)S(1)}, f32[512]{0:T(512)S(1)}) fusion(s32[512]{0:T(512)S(1)} %broadcast_subtract_fusion, bf16[512,3584]{1,0:T(8,128)(2,1)} %all-gather.28.cloned.1.call-done, bf16[3584,4096]{1,0:T(8,128)(2,1)} %param.33), kind=kOutput, calls=%fused_computation.2 | convolution fusion | flops 15044968448 | bytes 33036288 | tf_op jit(solution)/shard_map/dot_general | solution.py:118
  503.2 39.3 %psum.21 = f32[2,512]{1,0:T(2,128)S(1)} all-reduce(f32[2,512]{1,0:T(2,128)S(1)} %pad_maximum_fusion), channel_id=1, replica_groups=mesh['cand'=4,'tensor'=8] {'cand','tensor'}, use_global_device_ids=true, to_apply=%region_11.12 | all-reduce | flops 1024 | bytes 8192 | tf_op jit(solution)/shard_map/psum | solution.py:129
  542.6 1.2 fusion.52
  543.7 1.9 compare_select_fusion
  545.6 6.5 %all-reduce = (f32[4]{0:T(128)S(1)}, f32[4]{0:T(128)S(1)}) all-reduce(f32[4]{0:T(128)S(1)} %get-tuple-element.18, f32[4]{0:T(128)S(1)} %get-tuple-element.17), channel_id=1, replica_groups=mesh['cand'=4,'tensor'=8] {'cand'}, use_global_device_ids=true, to_apply=%region_13.14 | all-reduce | flops 8 | bytes 64 | tf_op jit(solution)/shard_map/psum | solution.py:134
  552.1 0.5 maximum_divide_fusion
  (56 shorter events, 3.0 us)
Async XLA Ops:
  7.2 4.4 copy-start.1
  7.2 26.2 %all-gather.16.cloned.1.call-start = ((), (), s32[]{:S(2)}) async-start(), calls=%async_computation.2 | async-start | bytes 2293760 | tf_op jit(solution)/shard_map/all_gather | solution.py:75
  9.2 46.9 %all-gather.18.cloned.1.call-start = ((), (), s32[]{:S(2)}) async-start(), calls=%async_computation.3 | async-start | bytes 2293760 | tf_op jit(solution)/shard_map/all_gather | solution.py:79
  11.5 77.6 %all-gather.22.cloned.1.call-start = ((), (), s32[]{:S(2)}) async-start(), calls=%async_computation.5 | async-start | bytes 4587520 | tf_op jit(solution)/shard_map/all_gather | solution.py:78
  13.1 5.0 copy-start.2
  13.2 108.9 %all-gather.20.cloned.1.call-start = ((), (), s32[]{:S(2)}) async-start(), calls=%async_computation.4 | async-start | bytes 4587520 | tf_op jit(solution)/shard_map/all_gather | solution.py:74
  13.7 130.9 %all-gather.12.cloned.1.call-start = ((), (), s32[]{:S(2)}) async-start(), calls=%async_computation | async-start | bytes 2293760 | tf_op jit(solution)/shard_map/all_gather | solution.py:76
  15.6 4.9 copy-start.8
  15.6 7.4 %copy-start.9 = (f32[4]{0:T(128)S(1)}, f32[4]{0:T(128)}, u32[]{:S(2)}) copy-start(f32[4]{0:T(128)} %param.21) | copy-start | bytes 52
  15.6 8.1 %copy-start = (bf16[128,3584]{1,0:T(8,128)(2,1)S(1)}, bf16[128,3584]{1,0:T(8,128)(2,1)}, u32[]{:S(2)}) copy-start(bf16[128,3584]{1,0:T(8,128)(2,1)} %param.17) | copy-start | bytes 2752516
  15.6 40.4 %copy-start.7 = (f32[3584]{0:T(1024)S(1)}, f32[3584]{0:T(1024)}, u32[]{:S(2)}) copy-start(f32[3584]{0:T(1024)} %param.30) | copy-start | bytes 43012
  15.7 151.5 %all-gather.14.cloned.1.call-start = ((), (), s32[]{:S(2)}) async-start(), calls=%async_computation.1 | async-start | bytes 2293760 | tf_op jit(solution)/shard_map/all_gather | solution.py:80
  18.1 182.1 %all-gather.26.cloned.1.call-start = ((), (), s32[]{:S(2)}) async-start(), calls=%async_computation.7 | async-start | bytes 4587520 | tf_op jit(solution)/shard_map/all_gather | solution.py:81
  19.7 213.6 %all-gather.24.cloned.1.call-start = ((), (), s32[]{:S(2)}) async-start(), calls=%async_computation.6 | async-start | bytes 4587520 | tf_op jit(solution)/shard_map/all_gather | solution.py:77
  20.4 421.2 %all-gather.30.cloned.1.call-start = ((), (), s32[]{:S(2)}) async-start(), calls=%async_computation.9 | async-start | bytes 16515072 | tf_op jit(solution)/shard_map/all_gather | solution.py:116
  239.8 240.5 %all-gather.28.cloned.1.call-start = ((), (), s32[]{:S(2)}) async-start(), calls=%async_computation.8 | async-start | bytes 4587520 | tf_op jit(solution)/shard_map/all_gather | solution.py:119
  441.7 6.9 %copy-start.3 = (f32[3584]{0:T(1024)S(1)}, f32[3584]{0:T(1024)}, u32[]{:S(2)}) copy-start(f32[3584]{0:T(1024)} %param.31) | copy-start | bytes 43012
  448.3 0.8 copy-start.4
  448.5 2.0 copy-start.5
  450.5 92.1 %copy-start.6 = (s32[128]{0:T(128)S(1)}, s32[128]{0:T(128)}, u32[]{:S(2)}) copy-start(s32[128]{0:T(128)} %param.19) | copy-start | bytes 1540
Sparse Core Ops, SparseCore 0:
  9.5 23.8 all-gather.15
  35.0 21.0 all-gather.17
  57.7 31.4 all-gather.21
  90.6 31.4 all-gather.19
  123.5 21.0 all-gather.11
  146.1 21.0 all-gather.13
  168.7 31.4 all-gather.25
  201.8 31.4 all-gather.23
  240.0 201.6 all-gather.29
  450.6 29.6 all-gather.27
